TPU v7x, 32 devices: a whole 2x2x4 slice. The times are simulated.
32 devices in a mesh: gx: 4 (over z), gy: 4 (over y, core), gz: 2 (over x).
Axes of the slice: x: 2, y: 2, z: 4, core: 2. Of those that a mesh axis runs over, the one named last changes fastest.
Arguments:
- right_side: float32 [128, 128, 256], P('gx', 'gy', 'gz'), may hold values from -8 to 8
- guess: float32 [128, 128, 256], P('gx', 'gy', 'gz'), may hold values from -4 to 4
Outputs:
- solution_field: float32 [128, 128, 256], P('gx', 'gy', 'gz')
- residual: float32 [128, 128, 256], P('gx', 'gy', 'gz')
All inputs are finite; a program needn't handle non-finite values.
Results may differ from a plain program's by a relative error of at most 0.0001.
Values sent between devices are 32-bit elements; how exact they have to be, the bound alone decides.
A program may use at most 128 MiB of HBM per device.

v0:
```python
import jax
import jax.numpy as jnp
from jax import lax
from jax.sharding import PartitionSpec as P

LEVELS = 6
SWEEPS = 4
STEPS = 2
damping = 2.0 / 3.0


def passed_along(value, axis, steps):
    count = lax.axis_size(axis)
    first, last = (max(0, -steps), min(count, count - steps))
    return lax.ppermute(value, axis, [(source, source + steps) for source in range(first, last)])


def padded_2(x, sides, width):
    for axis, dim in sides:
        count, length = (lax.axis_size(axis), x.shape[dim])
        up = [(i, (i + 1) % count) for i in range(count - 1)]
        down = [(j, i) for i, j in up]
        last = lax.slice_in_dim(x, length - width, length, axis=dim)
        first = lax.slice_in_dim(x, 0, width, axis=dim)
        before = lax.ppermute(last, axis, up)
        after = lax.ppermute(first, axis, down)
        x = jnp.concatenate([before, x, after], axis=dim)
    return x


def padded_stencil(padded):
    beside = padded[2:, 1:-1, 1:-1] + padded[:-2, 1:-1, 1:-1]
    beside = beside + padded[1:-1, 2:, 1:-1] + padded[1:-1, :-2, 1:-1]
    beside = beside + padded[1:-1, 1:-1, 2:] + padded[1:-1, 1:-1, :-2]
    return 6.0 * padded[1:-1, 1:-1, 1:-1] - beside


def restrict(field):
    first, second, third = field.shape
    blocks = field.reshape(first // 2, 2, second // 2, 2, third // 2, 2)
    return jnp.mean(blocks, axis=(1, 3, 5))


def prolong(field):
    first, second, third = field.shape
    spread = jnp.broadcast_to(field[:, None, :, None, :, None], (first, 2, second, 2, third, 2))
    return spread.reshape(first * 2, second * 2, third * 2)


def axis_layers(packed, axis_name, by):
    if axis_name == "gx":
        return passed_along(packed, "gx", by)
    if axis_name == "gy":
        return passed_along(packed, "gy", by)
    return passed_along(packed, "gz", by)


def extend_all(fields, margin):
    current = list(fields)
    for dim_index, axis_name in ((0, "gx"), (1, "gy"), (2, "gz")):
        lows = [lax.slice_in_dim(f, 0, margin, axis=dim_index) for f in current]
        highs = [
            lax.slice_in_dim(f, f.shape[dim_index] - margin, f.shape[dim_index], axis=dim_index)
            for f in current
        ]
        received = {}
        for by in (1, -1):
            pieces = highs if by == 1 else lows
            packed = jnp.concatenate([p.reshape(-1) for p in pieces])
            received[by] = axis_layers(packed, axis_name, by)
        grown = []
        offset = 0
        for index, field in enumerate(current):
            piece_shape = lows[index].shape
            count = lows[index].size
            from_lower = received[1][offset : offset + count].reshape(piece_shape)
            from_upper = received[-1][offset : offset + count].reshape(piece_shape)
            offset = offset + count
            grown.append(jnp.concatenate([from_lower, field, from_upper], axis=dim_index))
        current = grown
    return current


def smooth_merged(items):
    results = {}
    approxes = [damping * rhs / (6.0 * 0.25**lev) for rhs, lev in items]
    for sweep_index in range(SWEEPS - 1):
        padded_list = extend_all(approxes, 1)
        renewed = []
        for index, (rhs, lev) in enumerate(items):
            scaling = 0.25**lev
            diagonal_value = 6.0 * scaling
            renewed.append(
                approxes[index]
                + damping * (rhs - scaling * padded_stencil(padded_list[index])) / diagonal_value
            )
        approxes = renewed
    for index, (rhs, lev) in enumerate(items):
        results[lev] = approxes[index]
    return results


def precondition(residual):
    chain = [residual]
    for level_index in range(1, LEVELS):
        chain.append(restrict(chain[-1]))
    first_level = LEVELS - 1
    local_levels = list(range(first_level + 1))
    smoothed = smooth_merged([(chain[lev], lev) for lev in local_levels])
    correction = smoothed[first_level]
    for level_index in range(first_level - 1, -1, -1):
        correction = prolong(correction) + smoothed[level_index]
    return correction


def apply_fine(field):
    padded = padded_2(field, (("gx", 0), ("gy", 1), ("gz", 2)), 1)
    return padded_stencil(padded)


def shards(right_side, guess):
    solution_field = guess
    residual = right_side - apply_fine(guess)
    for step_index in range(STEPS):
        direction = precondition(residual)
        image = apply_fine(direction)
        along, curvature = lax.psum(
            (jnp.sum(residual * direction), jnp.sum(direction * image)), ("gx", "gy", "gz")
        )
        alpha = along / curvature
        solution_field = solution_field + alpha * direction
        residual = residual - alpha * image
    return (solution_field, residual)


def solution(mesh):
    placed = (P("gx", "gy", "gz"), P("gx", "gy", "gz"))
    return jax.shard_map(
        shards,
        mesh=mesh,
        in_specs=placed,
        out_specs=(P("gx", "gy", "gz"), P("gx", "gy", "gz")),
        check_vma=False,
    )
```

profile of v0, /device:TPU:0, one launch (start us, length us, event | category | flops | bytes accessed | tf_op | source)
XLA Modules:
  0.0 606.6 jit_solution(4249604036732145625)
XLA Ops:
  2.7 5.6 collective-permute-start.1
  17.2 4.5 collective-permute-start.5
  25.7 34.9 %reshape.1638 = f32[16,2,16,2,64,2]{5,4,3,2,1,0:T(8,128)} reshape(f32[32,32,128]{2,1,0:T(8,128)S(1)} %copy.405) | data formatting | bytes 1048576 | tf_op jit(solution)/shard_map/reshape | solution.py:40
  60.5 12.2 %reduce_sum.140 = f32[16,16,64]{2,1,0:T(8,128)S(1)} reduce(f32[16,2,16,2,64,2]{5,4,3,2,1,0:T(8,128)} %reshape.1638, f32[]{:T(128)} %constant.169.clone.1), dimensions={1,3,5}, to_apply=%region_0.0 | reduce | flops 114688 | bytes 589828 | tf_op jit(solution)/shard_map/reduce_sum | solution.py:41
  72.8 5.6 div.223
  97.4 5.7 collective-permute-done.8
  109.0 4.7 collective-permute-start.11
  128.3 4.4 collective-permute-done.12
  147.7 4.5 collective-permute-start.17
  170.4 4.4 collective-permute-done.18
  190.2 4.9 collective-permute-start.23
  204.2 4.9 reshape.1846
  210.7 11.4 %broadcast_in_dim.39 = f32[16,2,16,2,64,2]{5,4,3,2,1,0:T(8,128)} broadcast(f32[16,16,64]{2,1,0:T(8,128)S(1)} %fusion.112), dimensions={0,2,4} | broadcast | bytes 589824 | tf_op jit(solution)/shard_map/broadcast_in_dim | solution.py:46
  222.0 24.1 %reshape.1849 = f32[32,32,128]{2,1,0:T(8,128)S(1)} reshape(f32[16,2,16,2,64,2]{5,4,3,2,1,0:T(8,128)} %broadcast_in_dim.39) | data formatting | bytes 1048576 | tf_op jit(solution)/shard_map/reshape | solution.py:47
  250.0 4.5 collective-permute-start.25
  263.5 4.5 collective-permute-start.29
  271.1 45.0 %all-reduce.1 = (f32[]{:T(128)}, f32[]{:T(128)}) all-reduce(f32[]{:T(128)} %get-tuple-element.9, f32[]{:T(128)} %get-tuple-element.8), channel_id=1, replica_groups=mesh['gx'=4,'gy'=4,'gz'=2] {'gx','gy','gz'}, use_global_device_ids=true, to_apply=%region_7.0 | all-reduce | flops 2 | bytes 16 | tf_op jit(solution)/shard_map/psum | solution.py:127
  317.9 34.9 %reshape.1852 = f32[16,2,16,2,64,2]{5,4,3,2,1,0:T(8,128)} reshape(f32[32,32,128]{2,1,0:T(8,128)S(1)} %copy.511) | data formatting | bytes 1048576 | tf_op jit(solution)/shard_map/reshape | solution.py:40
  352.7 12.2 %reduce_sum.149 = f32[16,16,64]{2,1,0:T(8,128)S(1)} reduce(f32[16,2,16,2,64,2]{5,4,3,2,1,0:T(8,128)} %reshape.1852, f32[]{:T(128)} %constant.169.clone.1), dimensions={1,3,5}, to_apply=%region_10.0 | reduce | flops 114688 | bytes 589828 | tf_op jit(solution)/shard_map/reduce_sum | solution.py:41
  365.0 5.6 div.269
  378.1 4.3 collective-permute-done.30
  399.4 4.5 collective-permute-start.35
  416.4 4.3 collective-permute-done.36
  437.6 4.5 collective-permute-start.41
  455.9 4.4 collective-permute-done.42
  477.2 4.8 collective-permute-start.47
  488.1 4.9 reshape.2060
  493.8 11.4 %broadcast_in_dim.87 = f32[16,2,16,2,64,2]{5,4,3,2,1,0:T(8,128)} broadcast(f32[16,16,64]{2,1,0:T(8,128)S(1)} %fusion.81), dimensions={0,2,4} | broadcast | bytes 589824 | tf_op jit(solution)/shard_map/broadcast_in_dim | solution.py:46
  505.1 24.5 %reshape.2063 = f32[32,32,128]{2,1,0:T(8,128)} reshape(f32[16,2,16,2,64,2]{5,4,3,2,1,0:T(8,128)} %broadcast_in_dim.87) | data formatting | bytes 1048576 | tf_op jit(solution)/shard_map/reshape | solution.py:47
  533.8 4.5 collective-permute-start.49
  547.9 4.5 collective-permute-start.53
  556.4 44.8 %all-reduce = (f32[]{:T(128)}, f32[]{:T(128)}) all-reduce(f32[]{:T(128)} %get-tuple-element.7, f32[]{:T(128)} %get-tuple-element.6), channel_id=1, replica_groups=mesh['gx'=4,'gy'=4,'gz'=2] {'gx','gy','gz'}, use_global_device_ids=true, to_apply=%region_17.0 | all-reduce | flops 2 | bytes 16 | tf_op jit(solution)/shard_map/psum | solution.py:127
  (1040 shorter events, 240.0 us)
Async XLA Ops:
  1.4 8.2 %collective-permute-start = (f32[1,32,128]{2,0,1:T(1,128)S(1)}, f32[1,32,128]{2,0,1:T(1,128)S(1)}, u32[]{:S(2)}, u32[]{:S(2)}) collective-permute-start(f32[1,32,128]{2,0,1:T(1,128)S(1)} %bitcast.399), channel_id=1, source_target_pairs={{8,0},{16,8},{24,16},{9,1},{17,9},{25,17},{10,2},{18,10},{26,18},{... | collective-permute-start | bytes 49160 | tf_op jit(solution)/shard_map/ppermute | solution.py:26
  2.7 7.0 %collective-permute-start.1 = (f32[1,32,128]{2,0,1:T(1,128)S(1)}, f32[1,32,128]{2,0,1:T(1,128)S(1)}, u32[]{:S(2)}, u32[]{:S(2)}) collective-permute-start(f32[1,32,128]{2,0,1:T(1,128)S(1)} %bitcast.398), channel_id=1, source_target_pairs={{0,8},{8,16},{16,24},{1,9},{9,17},{17,25},{2,10},{10,18},{18,26},{... | collective-permute-start | bytes 49160 | tf_op jit(solution)/shard_map/ppermute | solution.py:25
  15.5 6.2 %collective-permute-start.4 = (f32[34,34,1]{1,2,0:T(1,128)S(1)}, f32[34,34,1]{1,2,0:T(1,128)S(1)}, u32[]{:S(2)}, u32[]{:S(2)}) collective-permute-start(f32[34,34,1]{1,2,0:T(1,128)S(1)} %copy.400), channel_id=1, source_target_pairs={{1,0},{3,2},{5,4},{7,6},{9,8},{11,10},{13,12},{15,14},{17,16},{19,... | collective-permute-start | bytes 13880 | tf_op jit(solution)/shard_map/ppermute | solution.py:26
  17.2 6.0 collective-permute-start.5
  82.3 5.9 collective-permute-start.7
  95.9 7.1 %collective-permute-start.8 = (f32[5964]{0:T(1024)S(1)}, f32[5964]{0:T(1024)S(1)}, u32[]{:S(2)}, u32[]{:S(2)}) collective-permute-start(f32[5964]{0:T(1024)S(1)} %concatenate.1027), channel_id=1, source_target_pairs={{2,0},{4,2},{6,4},{3,1},{5,3},{7,5},{10,8},{12,10},{14,12},{11,9},... | collective-permute-start | bytes 71576 | tf_op jit(solution)/shard_map/ppermute | solution.py:15
  106.6 7.2 %collective-permute-start.10 = (f32[1641]{0:T(1024)S(1)}, f32[1641]{0:T(1024)S(1)}, u32[]{:S(2)}, u32[]{:S(2)}) collective-permute-start(f32[1641]{0:T(1024)S(1)} %concatenate.1035), channel_id=1, source_target_pairs={{1,0},{3,2},{5,4},{7,6},{9,8},{11,10},{13,12},{15,14},{17,16},{19,... | collective-permute-start | bytes 19700 | tf_op jit(solution)/shard_map/ppermute | solution.py:15
  109.0 5.9 collective-permute-start.11
  122.3 5.9 collective-permute-start.13
  126.9 5.8 collective-permute-start.12
  145.3 7.0 %collective-permute-start.16 = (f32[1641]{0:T(1024)S(1)}, f32[1641]{0:T(1024)S(1)}, u32[]{:S(2)}, u32[]{:S(2)}) collective-permute-start(f32[1641]{0:T(1024)S(1)} %concatenate.1085), channel_id=1, source_target_pairs={{1,0},{3,2},{5,4},{7,6},{9,8},{11,10},{13,12},{15,14},{17,16},{19,... | collective-permute-start | bytes 19700 | tf_op jit(solution)/shard_map/ppermute | solution.py:15
  147.7 5.9 collective-permute-start.17
  163.2 7.2 %collective-permute-start.19 = (f32[5460]{0:T(1024)S(1)}, f32[5460]{0:T(1024)S(1)}, u32[]{:S(2)}, u32[]{:S(2)}) collective-permute-start(f32[5460]{0:T(1024)S(1)} %concatenate.1120), channel_id=1, source_target_pairs={{0,8},{8,16},{16,24},{1,9},{9,17},{17,25},{2,10},{10,18},{18,26},{... | collective-permute-start | bytes 65528 | tf_op jit(solution)/shard_map/ppermute | solution.py:15
  169.1 5.8 collective-permute-start.18
  187.7 7.4 %collective-permute-start.22 = (f32[1641]{0:T(1024)S(1)}, f32[1641]{0:T(1024)S(1)}, u32[]{:S(2)}, u32[]{:S(2)}) collective-permute-start(f32[1641]{0:T(1024)S(1)} %concatenate.1135), channel_id=1, source_target_pairs={{1,0},{3,2},{5,4},{7,6},{9,8},{11,10},{13,12},{15,14},{17,16},{19,... | collective-permute-start | bytes 19700 | tf_op jit(solution)/shard_map/ppermute | solution.py:15
  190.2 5.9 collective-permute-start.23
  248.7 5.9 collective-permute-start.24
  250.0 6.0 collective-permute-start.25
  261.8 6.2 %collective-permute-start.28 = (f32[34,34,1]{1,2,0:T(1,128)S(1)}, f32[34,34,1]{1,2,0:T(1,128)S(1)}, u32[]{:S(2)}, u32[]{:S(2)}) collective-permute-start(f32[34,34,1]{1,2,0:T(1,128)S(1)} %copy.506), channel_id=1, source_target_pairs={{1,0},{3,2},{5,4},{7,6},{9,8},{11,10},{13,12},{15,14},{17,16},{19,... | collective-permute-start | bytes 13880 | tf_op jit(solution)/shard_map/ppermute | solution.py:26
  263.5 6.0 collective-permute-start.29
  385.7 5.8 collective-permute-start.32
  397.0 7.0 %collective-permute-start.34 = (f32[1641]{0:T(1024)S(1)}, f32[1641]{0:T(1024)S(1)}, u32[]{:S(2)}, u32[]{:S(2)}) collective-permute-start(f32[1641]{0:T(1024)S(1)} %concatenate.1193), channel_id=1, source_target_pairs={{1,0},{3,2},{5,4},{7,6},{9,8},{11,10},{13,12},{15,14},{17,16},{19,... | collective-permute-start | bytes 19700 | tf_op jit(solution)/shard_map/ppermute | solution.py:15
  399.4 5.9 collective-permute-start.35
  435.2 7.0 %collective-permute-start.40 = (f32[1641]{0:T(1024)S(1)}, f32[1641]{0:T(1024)S(1)}, u32[]{:S(2)}, u32[]{:S(2)}) collective-permute-start(f32[1641]{0:T(1024)S(1)} %concatenate.1243), channel_id=1, source_target_pairs={{1,0},{3,2},{5,4},{7,6},{9,8},{11,10},{13,12},{15,14},{17,16},{19,... | collective-permute-start | bytes 19700 | tf_op jit(solution)/shard_map/ppermute | solution.py:15
  437.6 5.9 collective-permute-start.41
  454.5 5.8 collective-permute-start.42
  474.8 7.2 %collective-permute-start.46 = (f32[1641]{0:T(1024)S(1)}, f32[1641]{0:T(1024)S(1)}, u32[]{:S(2)}, u32[]{:S(2)}) collective-permute-start(f32[1641]{0:T(1024)S(1)} %concatenate.1293), channel_id=1, source_target_pairs={{1,0},{3,2},{5,4},{7,6},{9,8},{11,10},{13,12},{15,14},{17,16},{19,... | collective-permute-start | bytes 19700 | tf_op jit(solution)/shard_map/ppermute | solution.py:15
  477.2 5.9 collective-permute-start.47
  532.5 5.9 collective-permute-start.48
  533.8 6.0 collective-permute-start.49
  546.2 6.2 %collective-permute-start.52 = (f32[34,34,1]{1,2,0:T(1,128)S(1)}, f32[34,34,1]{1,2,0:T(1,128)S(1)}, u32[]{:S(2)}, u32[]{:S(2)}) collective-permute-start(f32[34,34,1]{1,2,0:T(1,128)S(1)} %copy.612), channel_id=1, source_target_pairs={{1,0},{3,2},{5,4},{7,6},{9,8},{11,10},{13,12},{15,14},{17,16},{19,... | collective-permute-start | bytes 13880 | tf_op jit(solution)/shard_map/ppermute | solution.py:26
  547.9 6.0 collective-permute-start.53
  (47 other events, 543.6 us)
where the time goes:
time: 617 us; the launch traced here: 607 us
  local copies, waits for them, and re-layouts  258 us (42%)
  starting transfers between devices  131 us (21%)
  blocking collectives  89.7 us (15%)
  waiting for transfers between devices  64.4 us (10%)
  other arithmetic  57.4 us (9%)
  between operations  6.56 us (1%)
    psum x2, blocking collectives, shards(): lax.psum((jnp.sum(residual * direction), jnp.sum(direction * image)), ('g...  89.7 us
    ppermute x36, starting transfers between devices, passed_along(): lax.ppermute(value, axis, [(source, source + steps) for source in range(f...  81.6 us
    reshape x2, local copies, waits for them, and re-layouts, restrict(): blocks = field.reshape(first // 2, 2, second // 2, 2, third // 2, 2)  69.7 us
    reshape x8, local copies, waits for them, and re-layouts, prolong(): return spread.reshape(first * 2, second * 2, third * 2)  58.9 us
    ppermute x36, waiting for transfers between devices, passed_along(): lax.ppermute(value, axis, [(source, source + steps) for source in range(f...  56 us
    ppermute x9, starting transfers between devices, padded_2(): before = lax.ppermute(last, axis, up)  37.4 us
    reduce_sum x12, other arithmetic, restrict(): return jnp.mean(blocks, axis=(1, 3, 5))  30.3 us
    broadcast_in_dim x12, local copies, waits for them, and re-layouts, prolong(): jnp.broadcast_to(field[:, None, :, None, :, None], (first, 2, second, 2,...  28.4 us
  transfers between devices with their start and end apart: 54, of which 27 were waited for; matrix products, arithmetic and copies ran while one was open for 3% of the time, Pallas kernels for 0%

commit v1 on v0

--- a/solution.py
+++ b/solution.py
@@ -124,8 +124,9 @@
     for step_index in range(STEPS):
         direction = precondition(residual)
         image = apply_fine(direction)
-        along, curvature = lax.psum(
-            (jnp.sum(residual * direction), jnp.sum(direction * image)), ("gx", "gy", "gz")
+        point_quarters_up = lambda local_block: lax.psum(lax.psum(local_block, ("gy", "gz")), "gx")
+        along, curvature = point_quarters_up(
+            (jnp.sum(residual * direction), jnp.sum(direction * image))
         )
         alpha = along / curvature
         solution_field = solution_field + alpha * direction

time: 617 us -> 582 us (0.943)
  blocking collectives: 89.7 us -> 56.8 us
    psum x2 -> x4, blocking collectives: 89.7 us -> 56.8 us  [the longest x2 34 us: shards(): lax.psum(local_block, ('gy', 'gz'))]
where the time goes in v1:
time: 582 us; the launch traced here: 572 us
  local copies, waits for them, and re-layouts  258 us (44%)
  starting transfers between devices  128 us (22%)
  waiting for transfers between devices  64.6 us (11%)
  other arithmetic  57.4 us (10%)
  blocking collectives  56.8 us (10%)
  between operations  6.5 us (1%)
    ppermute x36, starting transfers between devices, passed_along(): lax.ppermute(value, axis, [(source, source + steps) for source in range(f...  79.4 us
    reshape x2, local copies, waits for them, and re-layouts, restrict(): blocks = field.reshape(first // 2, 2, second // 2, 2, third // 2, 2)  69.7 us
    reshape x8, local copies, waits for them, and re-layouts, prolong(): return spread.reshape(first * 2, second * 2, third * 2)  58.9 us
    ppermute x36, waiting for transfers between devices, passed_along(): lax.ppermute(value, axis, [(source, source + steps) for source in range(f...  56.2 us
    ppermute x9, starting transfers between devices, padded_2(): before = lax.ppermute(last, axis, up)  37.4 us
    psum x2, blocking collectives, shards(): lax.psum(local_block, ('gy', 'gz'))  34 us
    reduce_sum x12, other arithmetic, restrict(): return jnp.mean(blocks, axis=(1, 3, 5))  30.3 us
    broadcast_in_dim x12, local copies, waits for them, and re-layouts, prolong(): jnp.broadcast_to(field[:, None, :, None, :, None], (first, 2, second, 2,...  28.4 us
  transfers between devices with their start and end apart: 54, of which 27 were waited for; matrix products, arithmetic and copies ran while one was open for 3% of the time, Pallas kernels for 0%

profile of v1, /device:TPU:0, one launch (start us, length us, event | category | flops | bytes accessed | tf_op | source)
XLA Modules:
  0.0 571.6 jit_solution(18115075936510995777)
XLA Ops:
  2.7 5.6 collective-permute-start.1
  17.2 4.5 collective-permute-start.5
  25.7 34.9 %reshape.1638 = f32[16,2,16,2,64,2]{5,4,3,2,1,0:T(8,128)} reshape(f32[32,32,128]{2,1,0:T(8,128)S(1)} %copy.405) | data formatting | bytes 1048576 | tf_op jit(solution)/shard_map/reshape | solution.py:40
  60.5 12.2 %reduce_sum.140 = f32[16,16,64]{2,1,0:T(8,128)S(1)} reduce(f32[16,2,16,2,64,2]{5,4,3,2,1,0:T(8,128)} %reshape.1638, f32[]{:T(128)} %constant.169.clone.1), dimensions={1,3,5}, to_apply=%region_0.0 | reduce | flops 114688 | bytes 589828 | tf_op jit(solution)/shard_map/reduce_sum | solution.py:41
  72.8 5.6 div.223
  97.4 5.7 collective-permute-done.8
  109.0 4.7 collective-permute-start.11
  147.7 4.5 collective-permute-start.17
  170.4 4.4 collective-permute-done.18
  190.2 4.9 collective-permute-start.23
  204.2 4.9 reshape.1846
  210.7 11.4 %broadcast_in_dim.39 = f32[16,2,16,2,64,2]{5,4,3,2,1,0:T(8,128)} broadcast(f32[16,16,64]{2,1,0:T(8,128)S(1)} %fusion.112), dimensions={0,2,4} | broadcast | bytes 589824 | tf_op jit(solution)/shard_map/broadcast_in_dim | solution.py:46
  222.0 24.1 %reshape.1849 = f32[32,32,128]{2,1,0:T(8,128)S(1)} reshape(f32[16,2,16,2,64,2]{5,4,3,2,1,0:T(8,128)} %broadcast_in_dim.39) | data formatting | bytes 1048576 | tf_op jit(solution)/shard_map/reshape | solution.py:47
  250.0 4.5 collective-permute-start.25
  263.5 4.5 collective-permute-start.29
  271.1 17.0 %all-reduce.1 = (f32[]{:T(128)}, f32[]{:T(128)}) all-reduce(f32[]{:T(128)} %get-tuple-element.9, f32[]{:T(128)} %get-tuple-element.8), channel_id=1, replica_groups=mesh['gx'=4,'gy'=4,'gz'=2] {'gy','gz'}, use_global_device_ids=true, to_apply=%region_7.0 | all-reduce | flops 2 | bytes 16 | tf_op jit(solution)/shard_map/psum | solution.py:127
  288.2 11.4 %all-reduce.3 = (f32[]{:T(128)}, f32[]{:T(128)}) all-reduce(f32[]{:T(128)} %get-tuple-element.96, f32[]{:T(128)} %get-tuple-element.97), channel_id=1, replica_groups=mesh['gx'=4,'gy'=4,'gz'=2] {'gx'}, use_global_device_ids=true, to_apply=%region_8.0 | all-reduce | flops 2 | bytes 16 | tf_op jit(solution)/shard_map/psum | solution.py:127
  301.4 34.9 %reshape.1852 = f32[16,2,16,2,64,2]{5,4,3,2,1,0:T(8,128)} reshape(f32[32,32,128]{2,1,0:T(8,128)S(1)} %copy.511) | data formatting | bytes 1048576 | tf_op jit(solution)/shard_map/reshape | solution.py:40
  336.3 12.2 %reduce_sum.149 = f32[16,16,64]{2,1,0:T(8,128)S(1)} reduce(f32[16,2,16,2,64,2]{5,4,3,2,1,0:T(8,128)} %reshape.1852, f32[]{:T(128)} %constant.169.clone.1), dimensions={1,3,5}, to_apply=%region_12.0 | reduce | flops 114688 | bytes 589828 | tf_op jit(solution)/shard_map/reduce_sum | solution.py:41
  348.5 5.6 div.269
  382.3 4.5 collective-permute-start.35
  399.0 4.4 collective-permute-done.36
  420.5 4.5 collective-permute-start.41
  437.5 4.4 collective-permute-done.42
  458.7 4.5 collective-permute-start.47
  469.6 4.9 reshape.2060
  475.3 11.4 %broadcast_in_dim.87 = f32[16,2,16,2,64,2]{5,4,3,2,1,0:T(8,128)} broadcast(f32[16,16,64]{2,1,0:T(8,128)S(1)} %fusion.81), dimensions={0,2,4} | broadcast | bytes 589824 | tf_op jit(solution)/shard_map/broadcast_in_dim | solution.py:46
  486.7 24.5 %reshape.2063 = f32[32,32,128]{2,1,0:T(8,128)} reshape(f32[16,2,16,2,64,2]{5,4,3,2,1,0:T(8,128)} %broadcast_in_dim.87) | data formatting | bytes 1048576 | tf_op jit(solution)/shard_map/reshape | solution.py:47
  515.3 4.5 collective-permute-start.49
  529.4 4.5 collective-permute-start.53
  537.9 17.0 %all-reduce = (f32[]{:T(128)}, f32[]{:T(128)}) all-reduce(f32[]{:T(128)} %get-tuple-element.7, f32[]{:T(128)} %get-tuple-element.6), channel_id=1, replica_groups=mesh['gx'=4,'gy'=4,'gz'=2] {'gy','gz'}, use_global_device_ids=true, to_apply=%region_19.0 | all-reduce | flops 2 | bytes 16 | tf_op jit(solution)/shard_map/psum | solution.py:127
  554.9 11.3 %all-reduce.2 = (f32[]{:T(128)}, f32[]{:T(128)}) all-reduce(f32[]{:T(128)} %get-tuple-element.94, f32[]{:T(128)} %get-tuple-element.95), channel_id=1, replica_groups=mesh['gx'=4,'gy'=4,'gz'=2] {'gx'}, use_global_device_ids=true, to_apply=%region_20.0 | all-reduce | flops 2 | bytes 16 | tf_op jit(solution)/shard_map/psum | solution.py:127
  (1042 shorter events, 246.9 us)
Async XLA Ops:
  1.4 8.2 %collective-permute-start = (f32[1,32,128]{2,0,1:T(1,128)S(1)}, f32[1,32,128]{2,0,1:T(1,128)S(1)}, u32[]{:S(2)}, u32[]{:S(2)}) collective-permute-start(f32[1,32,128]{2,0,1:T(1,128)S(1)} %bitcast.399), channel_id=1, source_target_pairs={{8,0},{16,8},{24,16},{9,1},{17,9},{25,17},{10,2},{18,10},{26,18},{... | collective-permute-start | bytes 49160 | tf_op jit(solution)/shard_map/ppermute | solution.py:26
  2.7 7.0 %collective-permute-start.1 = (f32[1,32,128]{2,0,1:T(1,128)S(1)}, f32[1,32,128]{2,0,1:T(1,128)S(1)}, u32[]{:S(2)}, u32[]{:S(2)}) collective-permute-start(f32[1,32,128]{2,0,1:T(1,128)S(1)} %bitcast.398), channel_id=1, source_target_pairs={{0,8},{8,16},{16,24},{1,9},{9,17},{17,25},{2,10},{10,18},{18,26},{... | collective-permute-start | bytes 49160 | tf_op jit(solution)/shard_map/ppermute | solution.py:25
  15.5 6.2 %collective-permute-start.4 = (f32[34,34,1]{1,2,0:T(1,128)S(1)}, f32[34,34,1]{1,2,0:T(1,128)S(1)}, u32[]{:S(2)}, u32[]{:S(2)}) collective-permute-start(f32[34,34,1]{1,2,0:T(1,128)S(1)} %copy.400), channel_id=1, source_target_pairs={{1,0},{3,2},{5,4},{7,6},{9,8},{11,10},{13,12},{15,14},{17,16},{19,... | collective-permute-start | bytes 13880 | tf_op jit(solution)/shard_map/ppermute | solution.py:26
  17.2 6.0 %collective-permute-start.5 = (f32[34,34,1]{1,2,0:T(1,128)S(1)}, f32[34,34,1]{1,2,0:T(1,128)S(1)}, u32[]{:S(2)}, u32[]{:S(2)}) collective-permute-start(f32[34,34,1]{1,2,0:T(1,128)S(1)} %copy.402), channel_id=1, source_target_pairs={{0,1},{2,3},{4,5},{6,7},{8,9},{10,11},{12,13},{14,15},{16,17},{18,... | collective-permute-start | bytes 13880 | tf_op jit(solution)/shard_map/ppermute | solution.py:25
  82.3 5.9 %collective-permute-start.7 = (f32[5460]{0:T(1024)S(1)}, f32[5460]{0:T(1024)S(1)}, u32[]{:S(2)}, u32[]{:S(2)}) collective-permute-start(f32[5460]{0:T(1024)S(1)} %concatenate.1020), channel_id=1, source_target_pairs={{0,8},{8,16},{16,24},{1,9},{9,17},{17,25},{2,10},{10,18},{18,26},{... | collective-permute-start | bytes 65528 | tf_op jit(solution)/shard_map/ppermute | solution.py:15
  95.9 7.1 %collective-permute-start.8 = (f32[5964]{0:T(1024)S(1)}, f32[5964]{0:T(1024)S(1)}, u32[]{:S(2)}, u32[]{:S(2)}) collective-permute-start(f32[5964]{0:T(1024)S(1)} %concatenate.1027), channel_id=1, source_target_pairs={{2,0},{4,2},{6,4},{3,1},{5,3},{7,5},{10,8},{12,10},{14,12},{11,9},... | collective-permute-start | bytes 71576 | tf_op jit(solution)/shard_map/ppermute | solution.py:15
  106.6 7.2 %collective-permute-start.10 = (f32[1641]{0:T(1024)S(1)}, f32[1641]{0:T(1024)S(1)}, u32[]{:S(2)}, u32[]{:S(2)}) collective-permute-start(f32[1641]{0:T(1024)S(1)} %concatenate.1035), channel_id=1, source_target_pairs={{1,0},{3,2},{5,4},{7,6},{9,8},{11,10},{13,12},{15,14},{17,16},{19,... | collective-permute-start | bytes 19700 | tf_op jit(solution)/shard_map/ppermute | solution.py:15
  109.0 5.9 %collective-permute-start.11 = (f32[1641]{0:T(1024)S(1)}, f32[1641]{0:T(1024)S(1)}, u32[]{:S(2)}, u32[]{:S(2)}) collective-permute-start(f32[1641]{0:T(1024)S(1)} %concatenate.1037), channel_id=1, source_target_pairs={{0,1},{2,3},{4,5},{6,7},{8,9},{10,11},{12,13},{14,15},{16,17},{18,... | collective-permute-start | bytes 19700 | tf_op jit(solution)/shard_map/ppermute | solution.py:15
  122.3 5.9 %collective-permute-start.13 = (f32[5460]{0:T(1024)S(1)}, f32[5460]{0:T(1024)S(1)}, u32[]{:S(2)}, u32[]{:S(2)}) collective-permute-start(f32[5460]{0:T(1024)S(1)} %concatenate.1070), channel_id=1, source_target_pairs={{0,8},{8,16},{16,24},{1,9},{9,17},{17,25},{2,10},{10,18},{18,26},{... | collective-permute-start | bytes 65528 | tf_op jit(solution)/shard_map/ppermute | solution.py:15
  126.9 5.8 %collective-permute-start.12 = (f32[5460]{0:T(1024)S(1)}, f32[5460]{0:T(1024)S(1)}, u32[]{:S(2)}, u32[]{:S(2)}) collective-permute-start(f32[5460]{0:T(1024)S(1)} %concatenate.1069), channel_id=1, source_target_pairs={{8,0},{16,8},{24,16},{9,1},{17,9},{25,17},{10,2},{18,10},{26,18},{... | collective-permute-start | bytes 65528 | tf_op jit(solution)/shard_map/ppermute | solution.py:15
  145.3 7.0 %collective-permute-start.16 = (f32[1641]{0:T(1024)S(1)}, f32[1641]{0:T(1024)S(1)}, u32[]{:S(2)}, u32[]{:S(2)}) collective-permute-start(f32[1641]{0:T(1024)S(1)} %concatenate.1085), channel_id=1, source_target_pairs={{1,0},{3,2},{5,4},{7,6},{9,8},{11,10},{13,12},{15,14},{17,16},{19,... | collective-permute-start | bytes 19700 | tf_op jit(solution)/shard_map/ppermute | solution.py:15
  147.7 5.9 %collective-permute-start.17 = (f32[1641]{0:T(1024)S(1)}, f32[1641]{0:T(1024)S(1)}, u32[]{:S(2)}, u32[]{:S(2)}) collective-permute-start(f32[1641]{0:T(1024)S(1)} %concatenate.1087), channel_id=1, source_target_pairs={{0,1},{2,3},{4,5},{6,7},{8,9},{10,11},{12,13},{14,15},{16,17},{18,... | collective-permute-start | bytes 19700 | tf_op jit(solution)/shard_map/ppermute | solution.py:15
  163.2 7.2 %collective-permute-start.19 = (f32[5460]{0:T(1024)S(1)}, f32[5460]{0:T(1024)S(1)}, u32[]{:S(2)}, u32[]{:S(2)}) collective-permute-start(f32[5460]{0:T(1024)S(1)} %concatenate.1120), channel_id=1, source_target_pairs={{0,8},{8,16},{16,24},{1,9},{9,17},{17,25},{2,10},{10,18},{18,26},{... | collective-permute-start | bytes 65528 | tf_op jit(solution)/shard_map/ppermute | solution.py:15
  169.1 5.8 %collective-permute-start.18 = (f32[5460]{0:T(1024)S(1)}, f32[5460]{0:T(1024)S(1)}, u32[]{:S(2)}, u32[]{:S(2)}) collective-permute-start(f32[5460]{0:T(1024)S(1)} %concatenate.1119), channel_id=1, source_target_pairs={{8,0},{16,8},{24,16},{9,1},{17,9},{25,17},{10,2},{18,10},{26,18},{... | collective-permute-start | bytes 65528 | tf_op jit(solution)/shard_map/ppermute | solution.py:15
  187.7 7.4 %collective-permute-start.22 = (f32[1641]{0:T(1024)S(1)}, f32[1641]{0:T(1024)S(1)}, u32[]{:S(2)}, u32[]{:S(2)}) collective-permute-start(f32[1641]{0:T(1024)S(1)} %concatenate.1135), channel_id=1, source_target_pairs={{1,0},{3,2},{5,4},{7,6},{9,8},{11,10},{13,12},{15,14},{17,16},{19,... | collective-permute-start | bytes 19700 | tf_op jit(solution)/shard_map/ppermute | solution.py:15
  190.2 5.9 %collective-permute-start.23 = (f32[1641]{0:T(1024)S(1)}, f32[1641]{0:T(1024)S(1)}, u32[]{:S(2)}, u32[]{:S(2)}) collective-permute-start(f32[1641]{0:T(1024)S(1)} %concatenate.1137), channel_id=1, source_target_pairs={{0,1},{2,3},{4,5},{6,7},{8,9},{10,11},{12,13},{14,15},{16,17},{18,... | collective-permute-start | bytes 19700 | tf_op jit(solution)/shard_map/ppermute | solution.py:15
  248.7 5.9 %collective-permute-start.24 = (f32[1,32,128]{2,0,1:T(1,128)S(1)}, f32[1,32,128]{2,0,1:T(1,128)S(1)}, u32[]{:S(2)}, u32[]{:S(2)}) collective-permute-start(f32[1,32,128]{2,0,1:T(1,128)S(1)} %get-tuple-element.153), channel_id=1, source_target_pairs={{8,0},{16,8},{24,16},{9,1},{17,9},{25,17},{10,2},{18,10},{26,18},{... | collective-permute-start | bytes 49160 | tf_op jit(solution)/shard_map/ppermute | solution.py:26
  250.0 6.0 %collective-permute-start.25 = (f32[1,32,128]{2,0,1:T(1,128)S(1)}, f32[1,32,128]{2,0,1:T(1,128)S(1)}, u32[]{:S(2)}, u32[]{:S(2)}) collective-permute-start(f32[1,32,128]{2,0,1:T(1,128)S(1)} %get-tuple-element.152), channel_id=1, source_target_pairs={{0,8},{8,16},{16,24},{1,9},{9,17},{17,25},{2,10},{10,18},{18,26},{... | collective-permute-start | bytes 49160 | tf_op jit(solution)/shard_map/ppermute | solution.py:25
  261.8 6.2 %collective-permute-start.28 = (f32[34,34,1]{1,2,0:T(1,128)S(1)}, f32[34,34,1]{1,2,0:T(1,128)S(1)}, u32[]{:S(2)}, u32[]{:S(2)}) collective-permute-start(f32[34,34,1]{1,2,0:T(1,128)S(1)} %copy.506), channel_id=1, source_target_pairs={{1,0},{3,2},{5,4},{7,6},{9,8},{11,10},{13,12},{15,14},{17,16},{19,... | collective-permute-start | bytes 13880 | tf_op jit(solution)/shard_map/ppermute | solution.py:26
  263.5 6.0 %collective-permute-start.29 = (f32[34,34,1]{1,2,0:T(1,128)S(1)}, f32[34,34,1]{1,2,0:T(1,128)S(1)}, u32[]{:S(2)}, u32[]{:S(2)}) collective-permute-start(f32[34,34,1]{1,2,0:T(1,128)S(1)} %copy.508), channel_id=1, source_target_pairs={{0,1},{2,3},{4,5},{6,7},{8,9},{10,11},{12,13},{14,15},{16,17},{18,... | collective-permute-start | bytes 13880 | tf_op jit(solution)/shard_map/ppermute | solution.py:25
  379.9 7.0 %collective-permute-start.34 = (f32[1641]{0:T(1024)S(1)}, f32[1641]{0:T(1024)S(1)}, u32[]{:S(2)}, u32[]{:S(2)}) collective-permute-start(f32[1641]{0:T(1024)S(1)} %concatenate.1193), channel_id=1, source_target_pairs={{1,0},{3,2},{5,4},{7,6},{9,8},{11,10},{13,12},{15,14},{17,16},{19,... | collective-permute-start | bytes 19700 | tf_op jit(solution)/shard_map/ppermute | solution.py:15
  382.3 5.9 %collective-permute-start.35 = (f32[1641]{0:T(1024)S(1)}, f32[1641]{0:T(1024)S(1)}, u32[]{:S(2)}, u32[]{:S(2)}) collective-permute-start(f32[1641]{0:T(1024)S(1)} %concatenate.1195), channel_id=1, source_target_pairs={{0,1},{2,3},{4,5},{6,7},{8,9},{10,11},{12,13},{14,15},{16,17},{18,... | collective-permute-start | bytes 19700 | tf_op jit(solution)/shard_map/ppermute | solution.py:15
  397.7 5.8 %collective-permute-start.36 = (f32[5460]{0:T(1024)S(1)}, f32[5460]{0:T(1024)S(1)}, u32[]{:S(2)}, u32[]{:S(2)}) collective-permute-start(f32[5460]{0:T(1024)S(1)} %concatenate.1227), channel_id=1, source_target_pairs={{8,0},{16,8},{24,16},{9,1},{17,9},{25,17},{10,2},{18,10},{26,18},{... | collective-permute-start | bytes 65528 | tf_op jit(solution)/shard_map/ppermute | solution.py:15
  417.9 7.2 %collective-permute-start.40 = (f32[1641]{0:T(1024)S(1)}, f32[1641]{0:T(1024)S(1)}, u32[]{:S(2)}, u32[]{:S(2)}) collective-permute-start(f32[1641]{0:T(1024)S(1)} %concatenate.1243), channel_id=1, source_target_pairs={{1,0},{3,2},{5,4},{7,6},{9,8},{11,10},{13,12},{15,14},{17,16},{19,... | collective-permute-start | bytes 19700 | tf_op jit(solution)/shard_map/ppermute | solution.py:15
  420.5 5.9 %collective-permute-start.41 = (f32[1641]{0:T(1024)S(1)}, f32[1641]{0:T(1024)S(1)}, u32[]{:S(2)}, u32[]{:S(2)}) collective-permute-start(f32[1641]{0:T(1024)S(1)} %concatenate.1245), channel_id=1, source_target_pairs={{0,1},{2,3},{4,5},{6,7},{8,9},{10,11},{12,13},{14,15},{16,17},{18,... | collective-permute-start | bytes 19700 | tf_op jit(solution)/shard_map/ppermute | solution.py:15
  436.1 5.8 %collective-permute-start.42 = (f32[5460]{0:T(1024)S(1)}, f32[5460]{0:T(1024)S(1)}, u32[]{:S(2)}, u32[]{:S(2)}) collective-permute-start(f32[5460]{0:T(1024)S(1)} %concatenate.1277), channel_id=1, source_target_pairs={{8,0},{16,8},{24,16},{9,1},{17,9},{25,17},{10,2},{18,10},{26,18},{... | collective-permute-start | bytes 65528 | tf_op jit(solution)/shard_map/ppermute | solution.py:15
  456.3 7.0 %collective-permute-start.46 = (f32[1641]{0:T(1024)S(1)}, f32[1641]{0:T(1024)S(1)}, u32[]{:S(2)}, u32[]{:S(2)}) collective-permute-start(f32[1641]{0:T(1024)S(1)} %concatenate.1293), channel_id=1, source_target_pairs={{1,0},{3,2},{5,4},{7,6},{9,8},{11,10},{13,12},{15,14},{17,16},{19,... | collective-permute-start | bytes 19700 | tf_op jit(solution)/shard_map/ppermute | solution.py:15
  458.7 5.9 %collective-permute-start.47 = (f32[1641]{0:T(1024)S(1)}, f32[1641]{0:T(1024)S(1)}, u32[]{:S(2)}, u32[]{:S(2)}) collective-permute-start(f32[1641]{0:T(1024)S(1)} %concatenate.1295), channel_id=1, source_target_pairs={{0,1},{2,3},{4,5},{6,7},{8,9},{10,11},{12,13},{14,15},{16,17},{18,... | collective-permute-start | bytes 19700 | tf_op jit(solution)/shard_map/ppermute | solution.py:15
  514.0 5.9 %collective-permute-start.48 = (f32[1,32,128]{2,0,1:T(1,128)S(1)}, f32[1,32,128]{2,0,1:T(1,128)S(1)}, u32[]{:S(2)}, u32[]{:S(2)}) collective-permute-start(f32[1,32,128]{2,0,1:T(1,128)S(1)} %get-tuple-element.145), channel_id=1, source_target_pairs={{8,0},{16,8},{24,16},{9,1},{17,9},{25,17},{10,2},{18,10},{26,18},{... | collective-permute-start | bytes 49160 | tf_op jit(solution)/shard_map/ppermute | solution.py:26
  515.3 6.0 %collective-permute-start.49 = (f32[1,32,128]{2,0,1:T(1,128)S(1)}, f32[1,32,128]{2,0,1:T(1,128)S(1)}, u32[]{:S(2)}, u32[]{:S(2)}) collective-permute-start(f32[1,32,128]{2,0,1:T(1,128)S(1)} %get-tuple-element.144), channel_id=1, source_target_pairs={{0,8},{8,16},{16,24},{1,9},{9,17},{17,25},{2,10},{10,18},{18,26},{... | collective-permute-start | bytes 49160 | tf_op jit(solution)/shard_map/ppermute | solution.py:25
  527.8 6.2 %collective-permute-start.52 = (f32[34,34,1]{1,2,0:T(1,128)S(1)}, f32[34,34,1]{1,2,0:T(1,128)S(1)}, u32[]{:S(2)}, u32[]{:S(2)}) collective-permute-start(f32[34,34,1]{1,2,0:T(1,128)S(1)} %copy.612), channel_id=1, source_target_pairs={{1,0},{3,2},{5,4},{7,6},{9,8},{11,10},{13,12},{15,14},{17,16},{19,... | collective-permute-start | bytes 13880 | tf_op jit(solution)/shard_map/ppermute | solution.py:26
  529.4 6.0 %collective-permute-start.53 = (f32[34,34,1]{1,2,0:T(1,128)S(1)}, f32[34,34,1]{1,2,0:T(1,128)S(1)}, u32[]{:S(2)}, u32[]{:S(2)}) collective-permute-start(f32[34,34,1]{1,2,0:T(1,128)S(1)} %copy.614), channel_id=1, source_target_pairs={{0,1},{2,3},{4,5},{6,7},{8,9},{10,11},{12,13},{14,15},{16,17},{18,... | collective-permute-start | bytes 13880 | tf_op jit(solution)/shard_map/ppermute | solution.py:25
  (47 other events, 541.2 us)
